TPU v7x, 32 devices: a whole 2x2x4 slice. The times are simulated.
32 devices in a mesh: dp: 8 (over y, x, core), mp: 4 (over z).
Axes of the slice: x: 2, y: 2, z: 4, core: 2. Of those that a mesh axis runs over, the one named last changes fastest.
Arguments:
- tokens: bfloat16 [16384, 1024], P(('dp', 'mp')), may hold values from -6 to 6
- norm_gain: float32 [2, 1024], replicated, may hold values from 0.1 to 1.9
- qkv_weight: bfloat16 [3, 1024, 1024], P(None, 'dp', 'mp')
- out_weight: bfloat16 [1024, 1024], P('mp', 'dp'), may hold values from -0.1875 to 0.1875
- variate_bias: float32 [2, 16], replicated, may hold values from -6 to 6
- ffn_weight: bfloat16 [2, 1024, 2816], P(None, 'dp', 'mp'), may hold values from -0.1875 to 0.1875
- down_weight: bfloat16 [2816, 1024], P('mp', 'dp'), may hold values from -0.109375 to 0.109375
- sample_ids: int32 [16384], P(('dp', 'mp')), may hold values from 0 to 127, as said below
- variate_ids: int32 [16384], P(('dp', 'mp')), may hold values from 0 to 15, as said below
- time_ids: int32 [16384], P(('dp', 'mp')), may hold values from 0 to 31, as said below
Outputs:
- encoded: bfloat16 [16384, 1024], P(('dp', 'mp'))
Inputs may be any that keep to these rules, and one draw needn't show every extreme that they name: `sample_ids`: within each packed sequence of 512 tokens the series numbers start at 0 and never fall; a series with v variates (1 to 16) and p patches (4 to 32) holds v * p consecutive tokens, the last series of a sequence may be cut short; some packed sequence holds 128 series of one variate and four patches each. `variate_ids`: A token's offset within its series divided by that series' patch count p. `time_ids`: A token's offset within its series modulo that series' patch count p.
All inputs are finite; a program needn't handle non-finite values.
Results may differ from a plain program's by a relative error of at most 0.017.
Values may be sent and summed in bfloat16 or wider, within the bound.
A program may use at most 128 MiB of HBM per device.

v0:
```python
import jax
import jax.numpy as jnp
from jax import lax
from jax.sharding import PartitionSpec as P

HEAD_DIM = 64
L = 512


def rms_norm(values, gain):
    wide = values.astype(jnp.float32)
    square = jnp.mean(wide * wide, axis=-1, keepdims=True)
    return (wide * lax.rsqrt(square + 1e-05) * gain[None, :]).astype(jnp.bfloat16)


def rotate(values, times):
    half = values.shape[-1] // 2
    freq = 10000.0 ** (-jnp.arange(half, dtype=jnp.float32) / half)
    angle = times.astype(jnp.float32)[:, None] * freq[None, :]
    cosine = jnp.cos(angle)[:, None, :]
    sine = jnp.sin(angle)[:, None, :]
    first = values[..., :half]
    second = values[..., half:]
    return jnp.concatenate(
        [first * cosine - second * sine, first * sine + second * cosine], axis=-1
    )


def rotated(raw, times):
    row_total, local_width = raw.shape
    turned = rotate(raw.reshape(row_total, local_width // HEAD_DIM, HEAD_DIM), times)
    return turned.reshape(row_total, local_width).astype(jnp.bfloat16)


def attend(queries, keys_rot, values, samples, variates, bias):
    row_total, local_width = queries.shape
    heads_here = local_width // HEAD_DIM
    count = row_total // L

    def one_sequence(args):
        qs, ks, vs, sample_row, variate_row = args
        scores = jnp.einsum(
            "qhd,khd->hqk", qs, ks, preferred_element_type=jnp.float32
        ) * HEAD_DIM ** (-0.5)
        same = variate_row[:, None] == variate_row[None, :]
        scores = scores + jnp.where(same[None], bias[0][:, None, None], bias[1][:, None, None])
        scores = jnp.where((sample_row[:, None] == sample_row[None, :])[None], scores, -1e30)
        top = jnp.max(scores, axis=2, keepdims=True)
        expo = jnp.exp(scores - top)
        weights = (expo / jnp.sum(expo, axis=2, keepdims=True)).astype(jnp.bfloat16)
        return jnp.einsum("hqk,khd->qhd", weights, vs, preferred_element_type=jnp.float32).astype(
            jnp.bfloat16
        )

    shape = (count, L, heads_here, HEAD_DIM)
    result = lax.map(
        one_sequence,
        (
            queries.reshape(shape),
            keys_rot.reshape(shape),
            values.reshape(shape),
            samples.reshape(count, L),
            variates.reshape(count, L),
        ),
    )
    return result.reshape(row_total, local_width)


def local(
    tokens,
    norm_gain,
    qkv_weight,
    out_weight,
    variate_bias,
    ffn_weight,
    down_weight,
    sample_ids,
    variate_ids,
    time_ids,
):
    heads_here = qkv_weight.shape[2] // HEAD_DIM
    head_start = lax.axis_index("mp") * heads_here
    bias_local = lax.dynamic_slice_in_dim(variate_bias, head_start, heads_here, 1)
    first_normed = rms_norm(tokens, norm_gain[0])
    wide_columns = lax.all_gather(qkv_weight, "mp", axis=2, tiled=True)
    columns = first_normed
    projected = jnp.einsum(
        "rc,jcd->jrd",
        columns,
        lax.all_gather(wide_columns, "dp", axis=1, tiled=True),
        preferred_element_type=jnp.float32,
    )
    queries = rotated(projected[0], time_ids)
    keys_rot = rotated(projected[1], time_ids)
    values = projected[2].astype(jnp.bfloat16)
    grouped = lax.all_to_all(
        jnp.stack([queries, keys_rot, values]), "mp", split_axis=2, concat_axis=1, tiled=True
    )
    gathered_ids = (
        lax.all_gather(sample_ids, "mp", axis=0, tiled=True),
        lax.all_gather(variate_ids, "mp", axis=0, tiled=True),
    )
    attended = attend(
        grouped[0], grouped[1], grouped[2], gathered_ids[0], gathered_ids[1], bias_local
    )
    back_rows = lax.all_to_all(attended, "mp", split_axis=0, concat_axis=1, tiled=True)
    out_rows = lax.all_gather(out_weight, "mp", axis=0, tiled=True)
    mixed = jnp.dot(
        back_rows,
        lax.all_gather(out_rows, "dp", axis=1, tiled=True),
        preferred_element_type=jnp.float32,
    )
    residual = (tokens.astype(jnp.float32) + mixed).astype(jnp.bfloat16)
    second_normed = rms_norm(residual, norm_gain[1])
    ffn_columns = lax.all_gather(ffn_weight, "mp", axis=2, tiled=True)
    columns = second_normed
    gate_up = jnp.einsum(
        "rc,jcf->jrf",
        columns,
        lax.all_gather(ffn_columns, "dp", axis=1, tiled=True),
        preferred_element_type=jnp.float32,
    )
    hidden = (jax.nn.silu(gate_up[0]) * gate_up[1]).astype(jnp.bfloat16)
    down_full = lax.all_gather(down_weight, "mp", axis=0, tiled=True)
    feed = jnp.dot(
        hidden,
        lax.all_gather(down_full, "dp", axis=1, tiled=True),
        preferred_element_type=jnp.float32,
    )
    return (residual.astype(jnp.float32) + feed).astype(jnp.bfloat16)


def solution(mesh):
    return jax.shard_map(
        local,
        mesh=mesh,
        in_specs=(
            P(("dp", "mp"), None),
            P(),
            P(None, "dp", "mp"),
            P("mp", "dp"),
            P(),
            P(None, "dp", "mp"),
            P("mp", "dp"),
            P(("dp", "mp")),
            P(("dp", "mp")),
            P(("dp", "mp")),
        ),
        out_specs=P(("dp", "mp"), None),
        check_vma=False,
    )
```

profile of v0, /device:TPU:0, one launch (start us, length us, event | category | flops | bytes accessed | tf_op | source)
XLA Modules:
  0.0 358.3 jit_solution(14907393396261247635)
XLA Ops:
  6.5 2.2 copy.40
  8.8 27.7 %all_gather.30 = bf16[3,128,1024]{2,1,0:T(8,128)(2,1)} all-gather(bf16[3,128,256]{2,1,0:T(8,128)(2,1)} %param.14), channel_id=1, replica_groups=mesh['dp'=8,'mp'=4] {'mp'}, dimensions={2}, use_global_device_ids=true | all-gather | bytes 983040 | tf_op jit(solution)/shard_map/all_gather | solution.py:85
  36.6 18.9 %all_gather.34 = bf16[1024,128]{1,0:T(8,128)(2,1)} all-gather(bf16[256,128]{1,0:T(8,128)(2,1)} %param.15), channel_id=1, replica_groups=mesh['dp'=8,'mp'=4] {'mp'}, dimensions={0}, use_global_device_ids=true | all-gather | bytes 327680 | tf_op jit(solution)/shard_map/all_gather | solution.py:107
  56.8 4.9 %copy.41 = bf16[2,128,2816]{2,1,0:T(8,128)(2,1)} copy(bf16[2,128,2816]{1,0,2:T(2,128)(2,1)} %all-gather.12.cloned.1.call-done) | data formatting | bytes 2883584 | tf_op jit(solution)/shard_map/all_gather | solution.py:115
  62.3 41.2 %all-gather.8.cloned.1.call-done = bf16[3,1024,1024]{2,1,0:T(8,128)(2,1)} async-done(((bf16[3,128,1024]{2,1,0:T(8,128)(2,1)}), bf16[3,1024,1024]{2,1,0:T(8,128)(2,1)}) %all-gather.8.cloned.1.call-update) | async-done | bytes 6291472 | tf_op jit(solution)/shard_map/all_gather | solution.py:90
  103.5 5.7 %convolution_bitcast_fusion.1 = f32[3,512,1024]{2,1,0:T(8,128)S(1)} fusion(bf16[3,1024,1024]{2,1,0:T(8,128)(2,1)} %all-gather.8.cloned.1.call-done, bf16[512,1024]{1,0:T(8,128)(2,1)S(1)} %copy-done.2, f32[1024]{0:T(1024)S(1)} %bitcast.128, f32[512]{0:T(512)S(1)} %add_rsqrt_fusion.1), kind=kOutput, calls=%fused_computation.54 | convolution fusion | flops 3223322624 | bytes 13637632 | tf_op jit(solution)/shard_map/rc,jcd->jrd/dot_general | solution.py:87
  110.4 2.4 fusion.80
  112.8 2.0 copy.34
  114.8 2.9 copy.35
  117.7 2.3 subtract_convert_fusion.1
  122.8 2.5 pad_maximum_fusion
  125.3 5.7 %copy.38 = bf16[3,512,1024]{1,0,2:T(4,128)(2,1)} copy(bf16[3,512,1024]{2,1,0:T(8,128)(2,1)S(1)} %pad_maximum_fusion) | data formatting | bytes 6291456 | tf_op jit(solution)/shard_map/stack | solution.py:97
  131.0 5.0 %all-to-all-start = ((bf16[3,512,1024]{1,0,2:T(4,128)(2,1)}), bf16[3,512,1024]{1,0,2:T(4,128)(2,1)}, u32[]{:S(2)}, u32[]{:S(2)}) async-start(bf16[3,512,1024]{1,0,2:T(4,128)(2,1)} %copy.38), calls=%async_computation | async-start | bytes 8388608 | tf_op jit(solution)/shard_map/all_to_all | solution.py:96
  136.1 106.7 %all_gather.38 = bf16[2816,128]{1,0:T(8,128)(2,1)} all-gather(bf16[704,128]{1,0:T(8,128)(2,1)S(1)} %copy-done.4), channel_id=1, replica_groups=mesh['dp'=8,'mp'=4] {'mp'}, dimensions={0}, use_global_device_ids=true | all-gather | bytes 901120 | tf_op jit(solution)/shard_map/all_gather | solution.py:124
  242.9 11.9 %all-gather.1 = s32[4,1,512]{2,1,0:T(1,128)S(1)} all-gather(s32[1,1,512]{2,1,0:T(1,128)S(1)} %bitcast.129), channel_id=1, replica_groups=mesh['dp'=8,'mp'=4] {'mp'}, dimensions={0}, use_global_device_ids=true | all-gather | bytes 10240 | tf_op jit(solution)/shard_map/all_gather | solution.py:101
  254.8 12.1 %all-gather = s32[4,1,512]{2,1,0:T(1,128)S(1)} all-gather(s32[1,1,512]{2,1,0:T(1,128)S(1)} %bitcast.130), channel_id=1, replica_groups=mesh['dp'=8,'mp'=4] {'mp'}, dimensions={0}, use_global_device_ids=true | all-gather | bytes 10240 | tf_op jit(solution)/shard_map/all_gather | solution.py:100
  267.0 3.2 copy.39
  270.2 1.5 fusion.81
  271.7 31.2 %while.10 = (s32[]{:T(128)}, bf16[4,512,4,64]{1,3,2,0:T(8,128)(2,1)}, bf16[4,512,4,64]{1,3,2,0:T(8,128)(2,1)}, s32[4,512]{1,0:T(4,128)S(1)}, bf16[4,512,4,64]{1,...) while((s32[]{:T(128)}, ...), condition=%wide.region_4.5_spmd, body=%wide.region_1.4_spmd.sunk | while | flops 416943104 | bytes 3179681 | solution.py:56
  272.2 3.0 fusion.100
  275.2 4.3 %fusion.101 = bf16[4,512,4,64]{1,3,2,0:T(8,128)(2,1)} fusion(bf16[4,512,4,64]{1,3,2,0:T(8,128)(2,1)} %get-tuple-element.154, s32[]{:T(128)} %get-tuple-element.153, f32[4,512]{1,0:T(4,128)S(1)} %fusion.100, bf16[4,512,4,64]{1,3,2,0:T(8,128)(2,1)} %get-tuple-element.164, f32[4]{0:T(128)S(1)} %get-tuple-element.140, f32[4]{0:T(128)S(1)} %get-tuple-element.141, ...), kind=kOutput, calls=%fused_computation.14.clone.1 | convolution fusion | flops 275909120 | bytes 1584128 | tf_op jit(solution)/shard_map/while/body/eval_jaxpr/hqk,khd->qhd/dot_general | solution.py:51
  280.0 3.0 fusion.100
  283.0 4.3 %fusion.101 = bf16[4,512,4,64]{1,3,2,0:T(8,128)(2,1)} fusion(bf16[4,512,4,64]{1,3,2,0:T(8,128)(2,1)} %get-tuple-element.154, s32[]{:T(128)} %get-tuple-element.153, f32[4,512]{1,0:T(4,128)S(1)} %fusion.100, bf16[4,512,4,64]{1,3,2,0:T(8,128)(2,1)} %get-tuple-element.164, f32[4]{0:T(128)S(1)} %get-tuple-element.140, f32[4]{0:T(128)S(1)} %get-tuple-element.141, ...), kind=kOutput, calls=%fused_computation.14.clone.1 | convolution fusion | flops 275909120 | bytes 1584128 | tf_op jit(solution)/shard_map/while/body/eval_jaxpr/hqk,khd->qhd/dot_general | solution.py:51
  287.8 3.0 fusion.100
  290.8 4.3 %fusion.101 = bf16[4,512,4,64]{1,3,2,0:T(8,128)(2,1)} fusion(bf16[4,512,4,64]{1,3,2,0:T(8,128)(2,1)} %get-tuple-element.154, s32[]{:T(128)} %get-tuple-element.153, f32[4,512]{1,0:T(4,128)S(1)} %fusion.100, bf16[4,512,4,64]{1,3,2,0:T(8,128)(2,1)} %get-tuple-element.164, f32[4]{0:T(128)S(1)} %get-tuple-element.140, f32[4]{0:T(128)S(1)} %get-tuple-element.141, ...), kind=kOutput, calls=%fused_computation.14.clone.1 | convolution fusion | flops 275909120 | bytes 1584128 | tf_op jit(solution)/shard_map/while/body/eval_jaxpr/hqk,khd->qhd/dot_general | solution.py:51
  295.6 3.0 fusion.100
  298.6 4.3 %fusion.101 = bf16[4,512,4,64]{1,3,2,0:T(8,128)(2,1)} fusion(bf16[4,512,4,64]{1,3,2,0:T(8,128)(2,1)} %get-tuple-element.154, s32[]{:T(128)} %get-tuple-element.153, f32[4,512]{1,0:T(4,128)S(1)} %fusion.100, bf16[4,512,4,64]{1,3,2,0:T(8,128)(2,1)} %get-tuple-element.164, f32[4]{0:T(128)S(1)} %get-tuple-element.140, f32[4]{0:T(128)S(1)} %get-tuple-element.141, ...), kind=kOutput, calls=%fused_computation.14.clone.1 | convolution fusion | flops 275909120 | bytes 1584128 | tf_op jit(solution)/shard_map/while/body/eval_jaxpr/hqk,khd->qhd/dot_general | solution.py:51
  302.9 3.7 %all-to-all-start.1 = ((bf16[4,512,256]{1,2,0:T(8,128)(2,1)}), bf16[4,512,256]{1,2,0:T(8,128)(2,1)S(1)}, u32[]{:S(2)}, u32[]{:S(2)}) async-start(bf16[4,512,256]{1,2,0:T(8,128)(2,1)} %bitcast.24), calls=%async_computation.1 | async-start | bytes 2097152 | tf_op jit(solution)/shard_map/all_to_all | solution.py:106
  306.7 18.6 %all-to-all-done.1 = bf16[4,512,256]{1,2,0:T(8,128)(2,1)S(1)} async-done(((bf16[4,512,256]{1,2,0:T(8,128)(2,1)}), bf16[4,512,256]{1,2,0:T(8,128)(2,1)S(1)}, u32[]{:S(2)}, u32[]{:S(2)}) %all-to-all-start.1) | async-done | bytes 1048608 | tf_op jit(solution)/shard_map/all_to_all | solution.py:106
  325.3 3.0 fusion.60
  328.3 13.2 %convolution_bitcast_fusion = f32[2,512,2816]{2,1,0:T(8,128)} fusion(bf16[2,1024,2816]{2,1,0:T(8,128)(2,1)} %all-gather.14.cloned.1.call-done, bf16[512,1024]{1,0:T(8,128)(2,1)S(1)} %get-tuple-element.84, f32[1024]{0:T(1024)S(1)} %bitcast.125, f32[512]{0:T(512)S(1)} %add_rsqrt_fusion), kind=kOutput, calls=%fused_computation.41 | convolution fusion | flops 5907677184 | bytes 24123392 | tf_op jit(solution)/shard_map/rc,jcf->jrf/dot_general | solution.py:117
  341.6 10.2 %fusion.63 = bf16[512,1024]{1,0:T(8,128)(2,1)} fusion(bf16[512,1024]{1,0:T(8,128)(2,1)S(1)} %get-tuple-element.84, bf16[2816,1024]{1,0:T(8,128)(2,1)} %all-gather.16.cloned.1.call-done, f32[2,512,2816]{2,1,0:T(8,128)} %convolution_bitcast_fusion), kind=kOutput, calls=%fused_computation.62 | convolution fusion | flops 2963013632 | bytes 19398656 | tf_op jit(solution)/shard_map/dot_general | solution.py:125
  (64 shorter events, 8.0 us)
Async XLA Ops:
  6.5 260.4 %copy-start = (f32[2,16]{1,0:T(2,128)S(1)}, f32[2,16]{1,0:T(2,128)}, u32[]{:S(2)}) copy-start(f32[2,16]{1,0:T(2,128)} %param.16) | copy-start | bytes 388
  6.5 55.1 %copy-start.8 = (s32[512]{0:T(512)S(1)}, s32[512]{0:T(512)}, u32[]{:S(2)}) copy-start(s32[512]{0:T(512)} %param.21) | copy-start | bytes 6148
  6.5 55.2 %copy-start.2 = (bf16[512,1024]{1,0:T(8,128)(2,1)S(1)}, bf16[512,1024]{1,0:T(8,128)(2,1)}, u32[]{:S(2)}) copy-start(bf16[512,1024]{1,0:T(8,128)(2,1)} %param.12) | copy-start | bytes 3145732
  6.5 50.2 %all-gather.12.cloned.1.call-start = ((), (), s32[]{:S(2)}) async-start(), calls=%async_computation.4 | async-start | bytes 1802240 | tf_op jit(solution)/shard_map/all_gather | solution.py:115
  8.7 53.3 %copy-start.5 = (f32[2,1024]{1,0:T(2,128)S(1)}, f32[2,1024]{1,0:T(2,128)}, u32[]{:S(2)}) copy-start(f32[2,1024]{1,0:T(2,128)} %param.13) | copy-start | bytes 24580
  8.8 94.8 %all-gather.8.cloned.1.call-start = ((), (), s32[]{:S(2)}) async-start(), calls=%async_computation.2 | async-start | bytes 7077888 | tf_op jit(solution)/shard_map/all_gather | solution.py:90
  36.5 270.2 %all-gather.10.cloned.1.call-start = ((), (), s32[]{:S(2)}) async-start(), calls=%async_computation.3 | async-start | bytes 2359296 | tf_op jit(solution)/shard_map/all_gather | solution.py:110
  55.5 272.8 %all-gather.14.cloned.1.call-start = ((), (), s32[]{:S(2)}) async-start(), calls=%async_computation.5 | async-start | bytes 12976128 | tf_op jit(solution)/shard_map/all_gather | solution.py:120
  131.0 5.1 %copy-start.4 = (bf16[704,128]{1,0:T(8,128)(2,1)S(1)}, bf16[704,128]{1,0:T(8,128)(2,1)}, u32[]{:S(2)}) copy-start(bf16[704,128]{1,0:T(8,128)(2,1)} %param.18) | copy-start | bytes 540676
  131.0 111.8 %copy-start.6 = (s32[512]{0:T(512)S(1)}, s32[512]{0:T(512)}, u32[]{:S(2)}) copy-start(s32[512]{0:T(512)} %param.20) | copy-start | bytes 6148
  131.0 123.8 %copy-start.7 = (s32[512]{0:T(512)S(1)}, s32[512]{0:T(512)}, u32[]{:S(2)}) copy-start(s32[512]{0:T(512)} %param.19) | copy-start | bytes 6148
  131.0 136.0 %all-to-all-start = ((bf16[3,512,1024]{1,0,2:T(4,128)(2,1)}), bf16[3,512,1024]{1,0,2:T(4,128)(2,1)}, u32[]{:S(2)}, u32[]{:S(2)}) async-start(bf16[3,512,1024]{1,0,2:T(4,128)(2,1)} %copy.38), calls=%async_computation | async-start | bytes 8388608 | tf_op jit(solution)/shard_map/all_to_all | solution.py:96
  136.0 205.6 %all-gather.16.cloned.1.call-start = ((), (), s32[]{:S(2)}) async-start(), calls=%async_computation.6 | async-start | bytes 6488064 | tf_op jit(solution)/shard_map/all_gather | solution.py:127
  271.7 53.6 %copy-start.3 = (bf16[512,1024]{1,0:T(8,128)(2,1)S(1)}, bf16[512,1024]{1,0:T(8,128)(2,1)}, u32[]{:S(2)}) copy-start(bf16[512,1024]{1,0:T(8,128)(2,1)} %param.12) | copy-start | bytes 3145732
  302.9 22.3 %all-to-all-start.1 = ((bf16[4,512,256]{1,2,0:T(8,128)(2,1)}), bf16[4,512,256]{1,2,0:T(8,128)(2,1)S(1)}, u32[]{:S(2)}, u32[]{:S(2)}) async-start(bf16[4,512,256]{1,2,0:T(8,128)(2,1)} %bitcast.24), calls=%async_computation.1 | async-start | bytes 2097152 | tf_op jit(solution)/shard_map/all_to_all | solution.py:106
  341.6 10.2 %copy-start.1 = (f32[2,16]{1,0:T(2,128)S(1)}, f32[2,16]{1,0:T(2,128)}, u32[]{:S(2)}) copy-start(f32[2,16]{1,0:T(2,128)} %param.16) | copy-start | bytes 388
Sparse Core Ops, SparseCore 0:
  8.9 47.8 all-gather.11
  58.7 44.7 all-gather.7
  105.4 28.0 all-gather.9
  135.3 67.5 all-gather.13
  243.0 44.4 all-gather.15
where the time goes:
time: 359 us; the launch traced here: 358 us
  blocking collectives  177 us (49%)
  matrix products  61.5 us (17%)
  waiting for transfers between devices  61.1 us (17%)
  local copies, waits for them, and re-layouts  28.7 us (8%)
  between operations  13.3 us (4%)
  starting transfers between devices  8.9 us (2%)
  other arithmetic  7.24 us (2%)
    all_gather x1, blocking collectives, local(): down_full = lax.all_gather(down_weight, 'mp', axis=0, tiled=True)  107 us
    all_gather x1, waiting for transfers between devices, local(): lax.all_gather(wide_columns, 'dp', axis=1, tiled=True)  41.2 us
    all_gather x1, blocking collectives, local(): wide_columns = lax.all_gather(qkv_weight, 'mp', axis=2, tiled=True)  27.7 us
    all_gather x1, blocking collectives, local(): out_rows = lax.all_gather(out_weight, 'mp', axis=0, tiled=True)  18.9 us
    all_to_all x1, waiting for transfers between devices, local(): lax.all_to_all(attended, 'mp', split_axis=0, concat_axis=1, tiled=True)  18.6 us
    dot_general x4, matrix products, one_sequence(): jnp.einsum('hqk,khd->qhd', weights, vs, preferred_element_type=jnp.float32)  17.2 us
    dot_general x1, matrix products, local(): jnp.einsum('rc,jcf->jrf', columns, lax.all_gather(ffn_columns, 'dp', axis...  13.2 us
    sub x4, matrix products, one_sequence(): expo = jnp.exp(scores - top)  12.1 us
  transfers between devices with their start and end apart: 7, of which 3 were waited for; matrix products, arithmetic and copies ran while one was open for 24% of the time, Pallas kernels for 0%

commit v1 on v0

--- a/solution.py
+++ b/solution.py
@@ -124,7 +124,7 @@
     down_full = lax.all_gather(down_weight, "mp", axis=0, tiled=True)
     feed = jnp.dot(
         hidden,
-        lax.all_gather(down_full, "dp", axis=1, tiled=True),
+        jnp.concatenate(lax.all_gather(down_full, "dp"), axis=1),
         preferred_element_type=jnp.float32,
     )
     return (residual.astype(jnp.float32) + feed).astype(jnp.bfloat16)

time: 359 us -> 336 us (0.936)
  waiting for transfers between devices: 61.1 us -> 38.3 us
  matrix products: 61.5 us -> 48.2 us
  local copies, waits for them, and re-layouts: 28.7 us -> 37.4 us
  blocking collectives: 177 us -> 182 us
    all_gather x1, blocking collectives: 11.9 us -> 99.2 us  [local(): lax.all_gather(variate_ids, 'mp', axis=0, tiled=True)]
    all_gather x1, blocking collectives: 107 us -> 27.9 us  [local(): down_full = lax.all_gather(down_weight, 'mp', axis=0, tiled=True)]
    all_gather x1, waiting for transfers between devices: 41.2 us -> 24.6 us  [local(): lax.all_gather(wide_columns, 'dp', axis=1, tiled=True)]
    reshape x0 -> x1, local copies, waits for them, and re-layouts: none -> 8.19 us  [local(): jnp.concatenate(lax.all_gather(down_full, 'dp'), axis=1)]
    dot_general x1, matrix products: 10.2 us -> 4.32 us  [local(): jnp.dot(hidden, jnp.concatenate(lax.all_gather(down_full, 'dp'), axis=1),...]
    all_to_all x1, waiting for transfers between devices: 18.6 us -> 13.5 us  [local(): lax.all_to_all(attended, 'mp', split_axis=0, concat_axis=1, tiled=True)]
    dot_general x1, matrix products: 13.2 us -> 9.27 us  [local(): jnp.einsum('rc,jcf->jrf', columns, lax.all_gather(ffn_columns, 'dp', axis...]
    all_gather x1, blocking collectives: 18.9 us -> 15 us  [local(): out_rows = lax.all_gather(out_weight, 'mp', axis=0, tiled=True)]
  transfers between devices with their start and end apart: 7 -> 7, of which waited for: 3 -> 2; matrix products, arithmetic and copies ran while one was open for 24% -> 23% of each run, Pallas kernels for 0% -> 0%
where the time goes in v1:
time: 336 us; the launch traced here: 335 us
  blocking collectives  182 us (54%)
  matrix products  48.2 us (14%)
  waiting for transfers between devices  38.3 us (11%)
  local copies, waits for them, and re-layouts  37.4 us (11%)
  between operations  13.4 us (4%)
  starting transfers between devices  8.91 us (3%)
  other arithmetic  6.94 us (2%)
    all_gather x1, blocking collectives, local(): lax.all_gather(variate_ids, 'mp', axis=0, tiled=True)  99.2 us
    all_gather x1, blocking collectives, local(): wide_columns = lax.all_gather(qkv_weight, 'mp', axis=2, tiled=True)  27.9 us
    all_gather x1, blocking collectives, local(): down_full = lax.all_gather(down_weight, 'mp', axis=0, tiled=True)  27.9 us
    all_gather x1, waiting for transfers between devices, local(): lax.all_gather(wide_columns, 'dp', axis=1, tiled=True)  24.6 us
    dot_general x4, matrix products, one_sequence(): jnp.einsum('hqk,khd->qhd', weights, vs, preferred_element_type=jnp.float32)  16.9 us
    all_gather x1, blocking collectives, local(): out_rows = lax.all_gather(out_weight, 'mp', axis=0, tiled=True)  15 us
    all_to_all x1, waiting for transfers between devices, local(): lax.all_to_all(attended, 'mp', split_axis=0, concat_axis=1, tiled=True)  13.5 us
    all_gather x1, blocking collectives, local(): lax.all_gather(sample_ids, 'mp', axis=0, tiled=True)  12.1 us
  transfers between devices with their start and end apart: 7, of which 2 were waited for; matrix products, arithmetic and copies ran while one was open for 23% of the time, Pallas kernels for 0%

profile of v1, /device:TPU:0, one launch (start us, length us, event | category | flops | bytes accessed | tf_op | source)
XLA Modules:
  0.0 335.3 jit_solution(1875265429823034141)
XLA Ops:
  6.5 2.1 copy.51
  8.8 27.9 %all_gather.33 = bf16[3,128,1024]{2,1,0:T(8,128)(2,1)} all-gather(bf16[3,128,256]{2,1,0:T(8,128)(2,1)} %param.14), channel_id=1, replica_groups=mesh['dp'=8,'mp'=4] {'mp'}, dimensions={2}, use_global_device_ids=true | all-gather | bytes 983040 | tf_op jit(solution)/shard_map/all_gather | solution.py:85
  36.7 27.9 %all_gather.41 = bf16[2816,128]{1,0:T(8,128)(2,1)} all-gather(bf16[704,128]{1,0:T(8,128)(2,1)} %param.18), channel_id=1, replica_groups=mesh['dp'=8,'mp'=4] {'mp'}, dimensions={0}, use_global_device_ids=true | all-gather | bytes 901120 | tf_op jit(solution)/shard_map/all_gather | solution.py:124
  64.7 15.0 %all_gather.37 = bf16[1024,128]{1,0:T(8,128)(2,1)} all-gather(bf16[256,128]{1,0:T(8,128)(2,1)S(1)} %copy-done.4), channel_id=1, replica_groups=mesh['dp'=8,'mp'=4] {'mp'}, dimensions={0}, use_global_device_ids=true | all-gather | bytes 327680 | tf_op jit(solution)/shard_map/all_gather | solution.py:107
  79.8 4.9 %copy.52 = bf16[2,128,2816]{2,1,0:T(8,128)(2,1)} copy(bf16[2,128,2816]{1,0,2:T(2,128)(2,1)} %all-gather.13.cloned.1.call-done) | data formatting | bytes 2883584 | tf_op jit(solution)/shard_map/all_gather | solution.py:115
  85.4 24.6 %all-gather.9.cloned.1.call-done = bf16[3,1024,1024]{2,1,0:T(8,128)(2,1)} async-done(((bf16[3,128,1024]{2,1,0:T(8,128)(2,1)}), bf16[3,1024,1024]{2,1,0:T(8,128)(2,1)}) %all-gather.9.cloned.1.call-update) | async-done | bytes 6291472 | tf_op jit(solution)/shard_map/all_gather | solution.py:90
  110.1 5.7 %convolution_bitcast_fusion.1 = f32[3,512,1024]{2,1,0:T(8,128)S(1)} fusion(bf16[3,1024,1024]{2,1,0:T(8,128)(2,1)} %all-gather.9.cloned.1.call-done, bf16[512,1024]{1,0:T(8,128)(2,1)S(1)} %copy-done.2, f32[1024]{0:T(1024)S(1)} %bitcast.125, f32[512]{0:T(512)S(1)} %add_rsqrt_fusion.1), kind=kOutput, calls=%fused_computation.53 | convolution fusion | flops 3223322624 | bytes 13637632 | tf_op jit(solution)/shard_map/rc,jcd->jrd/dot_general | solution.py:87
  116.9 2.4 fusion.80
  119.3 2.0 copy.45
  121.3 3.0 copy.46
  124.2 2.3 subtract_convert_fusion.1
  129.3 2.2 pad_maximum_fusion
  131.5 5.8 %copy.49 = bf16[3,512,1024]{1,0,2:T(4,128)(2,1)} copy(bf16[3,512,1024]{2,1,0:T(8,128)(2,1)S(1)} %pad_maximum_fusion) | data formatting | bytes 6291456 | tf_op jit(solution)/shard_map/stack | solution.py:97
  137.3 5.0 %all-to-all-start = ((bf16[3,512,1024]{1,0,2:T(4,128)(2,1)}), bf16[3,512,1024]{1,0,2:T(4,128)(2,1)}, u32[]{:S(2)}, u32[]{:S(2)}) async-start(bf16[3,512,1024]{1,0,2:T(4,128)(2,1)} %copy.49), calls=%async_computation | async-start | bytes 8388608 | tf_op jit(solution)/shard_map/all_to_all | solution.py:96
  142.3 99.2 %all-gather.2 = s32[4,1,512]{2,1,0:T(1,128)S(1)} all-gather(s32[1,1,512]{2,1,0:T(1,128)S(1)} %bitcast.126), channel_id=1, replica_groups=mesh['dp'=8,'mp'=4] {'mp'}, dimensions={0}, use_global_device_ids=true | all-gather | bytes 10240 | tf_op jit(solution)/shard_map/all_gather | solution.py:101
  241.5 12.1 %all-gather.1 = s32[4,1,512]{2,1,0:T(1,128)S(1)} all-gather(s32[1,1,512]{2,1,0:T(1,128)S(1)} %bitcast.127), channel_id=1, replica_groups=mesh['dp'=8,'mp'=4] {'mp'}, dimensions={0}, use_global_device_ids=true | all-gather | bytes 10240 | tf_op jit(solution)/shard_map/all_gather | solution.py:100
  253.7 3.0 copy.50
  257.9 27.1 %while.10 = (s32[]{:T(128)}, bf16[4,512,4,64]{1,3,2,0:T(8,128)(2,1)}, bf16[4,512,4,64]{1,3,2,0:T(8,128)(2,1)}, s32[4,512]{1,0:T(4,128)S(1)}, bf16[4,512,4,64]{1,...) while((s32[]{:T(128)}, ...), condition=%wide.region_4.5_spmd, body=%wide.region_1.4_spmd.sunk | while | flops 416943104 | bytes 3179681 | solution.py:56
  258.3 2.1 fusion.100
  260.4 4.2 %fusion.101 = bf16[4,512,4,64]{1,3,2,0:T(8,128)(2,1)} fusion(bf16[4,512,4,64]{1,3,2,0:T(8,128)(2,1)} %get-tuple-element.154, s32[]{:T(128)} %get-tuple-element.153, f32[4,512]{1,0:T(4,128)S(1)} %fusion.100, bf16[4,512,4,64]{1,3,2,0:T(8,128)(2,1)} %get-tuple-element.164, f32[4]{0:T(128)S(1)} %get-tuple-element.140, f32[4]{0:T(128)S(1)} %get-tuple-element.141, ...), kind=kOutput, calls=%fused_computation.14.clone.1 | convolution fusion | flops 275909120 | bytes 1584128 | tf_op jit(solution)/shard_map/while/body/eval_jaxpr/hqk,khd->qhd/dot_general | solution.py:51
  265.1 2.1 fusion.100
  267.2 4.2 %fusion.101 = bf16[4,512,4,64]{1,3,2,0:T(8,128)(2,1)} fusion(bf16[4,512,4,64]{1,3,2,0:T(8,128)(2,1)} %get-tuple-element.154, s32[]{:T(128)} %get-tuple-element.153, f32[4,512]{1,0:T(4,128)S(1)} %fusion.100, bf16[4,512,4,64]{1,3,2,0:T(8,128)(2,1)} %get-tuple-element.164, f32[4]{0:T(128)S(1)} %get-tuple-element.140, f32[4]{0:T(128)S(1)} %get-tuple-element.141, ...), kind=kOutput, calls=%fused_computation.14.clone.1 | convolution fusion | flops 275909120 | bytes 1584128 | tf_op jit(solution)/shard_map/while/body/eval_jaxpr/hqk,khd->qhd/dot_general | solution.py:51
  271.9 2.1 fusion.100
  274.0 4.2 %fusion.101 = bf16[4,512,4,64]{1,3,2,0:T(8,128)(2,1)} fusion(bf16[4,512,4,64]{1,3,2,0:T(8,128)(2,1)} %get-tuple-element.154, s32[]{:T(128)} %get-tuple-element.153, f32[4,512]{1,0:T(4,128)S(1)} %fusion.100, bf16[4,512,4,64]{1,3,2,0:T(8,128)(2,1)} %get-tuple-element.164, f32[4]{0:T(128)S(1)} %get-tuple-element.140, f32[4]{0:T(128)S(1)} %get-tuple-element.141, ...), kind=kOutput, calls=%fused_computation.14.clone.1 | convolution fusion | flops 275909120 | bytes 1584128 | tf_op jit(solution)/shard_map/while/body/eval_jaxpr/hqk,khd->qhd/dot_general | solution.py:51
  278.7 2.1 fusion.100
  280.8 4.2 %fusion.101 = bf16[4,512,4,64]{1,3,2,0:T(8,128)(2,1)} fusion(bf16[4,512,4,64]{1,3,2,0:T(8,128)(2,1)} %get-tuple-element.154, s32[]{:T(128)} %get-tuple-element.153, f32[4,512]{1,0:T(4,128)S(1)} %fusion.100, bf16[4,512,4,64]{1,3,2,0:T(8,128)(2,1)} %get-tuple-element.164, f32[4]{0:T(128)S(1)} %get-tuple-element.140, f32[4]{0:T(128)S(1)} %get-tuple-element.141, ...), kind=kOutput, calls=%fused_computation.14.clone.1 | convolution fusion | flops 275909120 | bytes 1584128 | tf_op jit(solution)/shard_map/while/body/eval_jaxpr/hqk,khd->qhd/dot_general | solution.py:51
  285.0 3.7 %all-to-all-start.1 = ((bf16[4,512,256]{1,2,0:T(8,128)(2,1)}), bf16[4,512,256]{1,2,0:T(8,128)(2,1)S(1)}, u32[]{:S(2)}, u32[]{:S(2)}) async-start(bf16[4,512,256]{1,2,0:T(8,128)(2,1)} %bitcast.24), calls=%async_computation.1 | async-start | bytes 2097152 | tf_op jit(solution)/shard_map/all_to_all | solution.py:106
  288.8 8.2 %copy.53 = bf16[2816,8,128]{0,2,1:T(8,128)(2,1)} copy(bf16[2816,8,128]{2,0,1:T(8,128)(2,1)} %bitcast.110) | data formatting | bytes 11534336 | tf_op jit(solution)/shard_map/reshape | solution.py:127
  297.0 13.5 %all-to-all-done.1 = bf16[4,512,256]{1,2,0:T(8,128)(2,1)S(1)} async-done(((bf16[4,512,256]{1,2,0:T(8,128)(2,1)}), bf16[4,512,256]{1,2,0:T(8,128)(2,1)S(1)}, u32[]{:S(2)}, u32[]{:S(2)}) %all-to-all-start.1) | async-done | bytes 1048608 | tf_op jit(solution)/shard_map/all_to_all | solution.py:106
  311.4 3.7 %fusion.60 = (f32[512]{0:T(512)S(1)}, bf16[512,1024]{1,0:T(8,128)(2,1)S(1)}) fusion(bf16[512,1024]{0,1:T(8,128)(2,1)} %bitcast.116, bf16[1024,1024]{1,0:T(8,128)(2,1)} %all-gather.11.cloned.1.call-done, bf16[512,1024]{1,0:T(8,128)(2,1)} %param.12), kind=kOutput, calls=%fused_computation.58 | convolution fusion | flops 1076887040 | bytes 5244928 | tf_op jit(solution)/shard_map/dot_general | solution.py:108
  315.2 9.3 %convolution_bitcast_fusion = f32[2,512,2816]{2,1,0:T(8,128)S(1)} fusion(bf16[2,1024,2816]{2,1,0:T(8,128)(2,1)} %all-gather.15.cloned.1.call-done, bf16[512,1024]{1,0:T(8,128)(2,1)S(1)} %get-tuple-element.84, f32[1024]{0:T(1024)S(1)} %bitcast.122, f32[512]{0:T(512)S(1)} %add_rsqrt_fusion), kind=kOutput, calls=%fused_computation.41 | convolution fusion | flops 5907677184 | bytes 24123392 | tf_op jit(solution)/shard_map/rc,jcf->jrf/dot_general | solution.py:117
  324.5 4.3 %fusion.63 = bf16[512,1024]{1,0:T(8,128)(2,1)} fusion(bf16[512,1024]{1,0:T(8,128)(2,1)S(1)} %get-tuple-element.84, bf16[2816,1024]{0,1:T(8,128)(2,1)S(1)} %bitcast.113, f32[2,512,2816]{2,1,0:T(8,128)S(1)} %convolution_bitcast_fusion), kind=kOutput, calls=%fused_computation.61 | convolution fusion | flops 2963013632 | bytes 19398656 | tf_op jit(solution)/shard_map/dot_general | solution.py:125
  (70 shorter events, 8.9 us)
Async XLA Ops:
  6.5 247.1 %copy-start = (f32[2,16]{1,0:T(2,128)S(1)}, f32[2,16]{1,0:T(2,128)}, u32[]{:S(2)}) copy-start(f32[2,16]{1,0:T(2,128)} %param.16) | copy-start | bytes 388
  6.5 58.1 %copy-start.4 = (bf16[256,128]{1,0:T(8,128)(2,1)S(1)}, bf16[256,128]{1,0:T(8,128)(2,1)}, u32[]{:S(2)}) copy-start(bf16[256,128]{1,0:T(8,128)(2,1)} %param.15) | copy-start | bytes 196612
  6.5 73.3 %all-gather.13.cloned.1.call-start = ((), (), s32[]{:S(2)}) async-start(), calls=%async_computation.4 | async-start | bytes 1802240 | tf_op jit(solution)/shard_map/all_gather | solution.py:115
  8.7 76.1 %copy-start.8 = (s32[512]{0:T(512)S(1)}, s32[512]{0:T(512)}, u32[]{:S(2)}) copy-start(s32[512]{0:T(512)} %param.21) | copy-start | bytes 6148
  8.7 76.1 %copy-start.2 = (bf16[512,1024]{1,0:T(8,128)(2,1)S(1)}, bf16[512,1024]{1,0:T(8,128)(2,1)}, u32[]{:S(2)}) copy-start(bf16[512,1024]{1,0:T(8,128)(2,1)} %param.12) | copy-start | bytes 3145732
  8.7 101.3 %all-gather.9.cloned.1.call-start = ((), (), s32[]{:S(2)}) async-start(), calls=%async_computation.2 | async-start | bytes 7077888 | tf_op jit(solution)/shard_map/all_gather | solution.py:90
  36.7 48.4 %copy-start.5 = (f32[2,1024]{1,0:T(2,128)S(1)}, f32[2,1024]{1,0:T(2,128)}, u32[]{:S(2)}) copy-start(f32[2,1024]{1,0:T(2,128)} %param.13) | copy-start | bytes 24580
  36.7 252.1 %all-gather.17.cloned.1.call-start = ((), (), s32[]{:S(2)}) async-start(), calls=%async_computation.6 | async-start | bytes 6488064 | tf_op jit(solution)/shard_map/all_gather | solution.py:127
  64.6 232.3 %all-gather.11.cloned.1.call-start = ((), (), s32[]{:S(2)}) async-start(), calls=%async_computation.3 | async-start | bytes 2359296 | tf_op jit(solution)/shard_map/all_gather | solution.py:110
  79.8 235.4 %all-gather.15.cloned.1.call-start = ((), (), s32[]{:S(2)}) async-start(), calls=%async_computation.5 | async-start | bytes 12976128 | tf_op jit(solution)/shard_map/all_gather | solution.py:120
  137.3 5.0 %copy-start.6 = (s32[512]{0:T(512)S(1)}, s32[512]{0:T(512)}, u32[]{:S(2)}) copy-start(s32[512]{0:T(512)} %param.20) | copy-start | bytes 6148
  137.3 104.2 %copy-start.7 = (s32[512]{0:T(512)S(1)}, s32[512]{0:T(512)}, u32[]{:S(2)}) copy-start(s32[512]{0:T(512)} %param.19) | copy-start | bytes 6148
  137.3 116.4 %all-to-all-start = ((bf16[3,512,1024]{1,0,2:T(4,128)(2,1)}), bf16[3,512,1024]{1,0,2:T(4,128)(2,1)}, u32[]{:S(2)}, u32[]{:S(2)}) async-start(bf16[3,512,1024]{1,0,2:T(4,128)(2,1)} %copy.49), calls=%async_computation | async-start | bytes 8388608 | tf_op jit(solution)/shard_map/all_to_all | solution.py:96
  285.0 25.5 %all-to-all-start.1 = ((bf16[4,512,256]{1,2,0:T(8,128)(2,1)}), bf16[4,512,256]{1,2,0:T(8,128)(2,1)S(1)}, u32[]{:S(2)}, u32[]{:S(2)}) async-start(bf16[4,512,256]{1,2,0:T(8,128)(2,1)} %bitcast.24), calls=%async_computation.1 | async-start | bytes 2097152 | tf_op jit(solution)/shard_map/all_to_all | solution.py:106
  310.5 1.0 copy-start.3
  311.4 13.0 %slice-start = ((s8[5767168]{0:T(1024)(128)(4,1)}), s8[1572864]{0:T(1024)(128)(4,1)S(1)}, s32[]{:S(2)}) async-start(s8[5767168]{0:T(1024)(128)(4,1)} %bitcast.111), calls=%async_computation.7 | async-start | bytes 3145728
  315.2 9.3 %slice-start.1 = ((s8[5767168]{0:T(1024)(128)(4,1)}), s8[4194304]{0:T(1024)(128)(4,1)S(1)}, s32[]{:S(2)}) async-start(s8[5767168]{0:T(1024)(128)(4,1)} %bitcast.111), calls=%async_computation.8 | async-start | bytes 8388608
  324.5 4.3 %copy-start.1 = (f32[2,16]{1,0:T(2,128)S(1)}, f32[2,16]{1,0:T(2,128)}, u32[]{:S(2)}) copy-start(f32[2,16]{1,0:T(2,128)} %param.16) | copy-start | bytes 388
Sparse Core Ops, SparseCore 0:
  8.9 54.3 all-gather.12
  65.2 44.7 all-gather.8
  111.9 43.1 all-gather.16
  156.9 28.0 all-gather.10
  186.8 67.5 all-gather.14
